TPU v7x, 128 devices: a whole 4x4x4 slice. The times are simulated.
128 devices in a mesh: kz: 4 (over z), jy: 4 (over y), ix: 8 (over x, core).
Axes of the slice: x: 4, y: 4, z: 4, core: 2. Of those that a mesh axis runs over, the one named last changes fastest.
Arguments:
- tensor: float32 [1536, 128, 1536], P('ix', 'jy', 'kz')
- b_init: float32 [128, 64], P(('jy', 'ix', 'kz'))
- c_init: float32 [1536, 64], P(('kz', 'ix', 'jy'))
- ridge: float32 [], replicated
Outputs:
- output 1: float32 [1536, 64], P(('ix', 'jy', 'kz'))
- output 2: float32 [128, 64], P(('jy', 'ix', 'kz'))
- output 3: float32 [1536, 64], P(('kz', 'ix', 'jy'))
- output 4: float32 [64], replicated
All inputs are finite; a program needn't handle non-finite values.
Results may differ from a plain program's by a relative error of at most 0.001.
Values are sent between devices in bfloat16 or wider.
A program may use at most 1 GiB of HBM per device.

v0:
```python
import jax
import jax.numpy as jnp
from jax import lax
from jax.sharding import PartitionSpec as P

SWEEPS = 2
ALL_AXES = ('kz', 'jy', 'ix')


def mat_prod(form, left, right):
    return jnp.einsum(form, left, right, precision=lax.Precision.HIGHEST, preferred_element_type=jnp.float32)


def gram_part(factor):
    return mat_prod('ir,is->rs', factor, factor)


def spd_inverse(system):
    rank_size = system.shape[0]
    row_ids = lax.broadcasted_iota(jnp.int32, (rank_size, 1), 0)

    def value_a9(col_idx, state_pair):
        left_mat, right_mat = state_pair
        pivot_left = lax.dynamic_slice_in_dim(left_mat, col_idx, 1, axis=0)
        pivot_right = lax.dynamic_slice_in_dim(right_mat, col_idx, 1, axis=0)
        pivot_val = lax.dynamic_slice_in_dim(pivot_left, col_idx, 1, axis=1)
        row_left = pivot_left / pivot_val
        row_right = pivot_right / pivot_val
        col_vals = lax.dynamic_slice_in_dim(left_mat, col_idx, 1, axis=1)
        is_pivot = row_ids == col_idx
        left_mat = jnp.where(is_pivot, row_left, left_mat - col_vals * row_left)
        right_mat = jnp.where(is_pivot, row_right, right_mat - col_vals * row_right)
        return left_mat, right_mat

    unused_left, inverse = lax.fori_loop(0, rank_size, value_a9, (system, jnp.eye(rank_size, dtype=jnp.float32)))
    return inverse


def solve_rows(mttkrp, gram_one, gram_two, ridge):
    rank_size = mttkrp.shape[1]
    system = gram_one * gram_two + ridge * jnp.eye(rank_size, dtype=jnp.float32)
    return mat_prod('ir,rs->is', mttkrp, spd_inverse(system))


def normalise(raw_rows, gram_raw):
    col_norms = jnp.sqrt(jnp.diagonal(gram_raw))
    return raw_rows / col_norms[None, :], gram_raw / (col_norms[:, None] * col_norms[None, :]), col_norms


def solution(mesh):
    def body(x_blk, b_loc, c_loc, ridge):
        gram_pair = lax.psum(jnp.stack([gram_part(b_loc), gram_part(c_loc)]), ALL_AXES)
        gram_b = gram_pair[0]
        gram_c = gram_pair[1]
        b_rows = lax.all_gather(b_loc, ('ix', 'kz'), axis=0, tiled=True)
        a_loc = None
        col_norms = None
        for sweep_idx in range(SWEEPS):
            c_rows = lax.all_gather(c_loc, ('ix', 'jy'), axis=0, tiled=True)
            t_ijr = mat_prod('ijk,kr->ijr', x_blk, c_rows)
            part_a = mat_prod('ijr,jr->ir', t_ijr, b_rows)
            m_a = lax.psum_scatter(part_a, ('jy', 'kz'), scatter_dimension=0, tiled=True)
            a_raw = solve_rows(m_a, gram_b, gram_c, ridge)
            a_loc, gram_a, col_norms = normalise(a_raw, lax.psum(gram_part(a_raw), ALL_AXES))
            a_rows = lax.all_gather(a_loc, ('jy', 'kz'), axis=0, tiled=True)
            part_b = mat_prod('ijr,ir->jr', t_ijr, a_rows)
            m_b = lax.psum_scatter(part_b, ('ix', 'kz'), scatter_dimension=0, tiled=True)
            b_raw = solve_rows(m_b, gram_a, gram_c, ridge)
            b_loc, gram_b, col_norms = normalise(b_raw, lax.psum(gram_part(b_raw), ALL_AXES))
            b_rows = lax.all_gather(b_loc, ('ix', 'kz'), axis=0, tiled=True)
            t_ikr = mat_prod('ijk,jr->ikr', x_blk, b_rows)
            part_c = mat_prod('ikr,ir->kr', t_ikr, a_rows)
            m_c = lax.psum_scatter(part_c, ('ix', 'jy'), scatter_dimension=0, tiled=True)
            c_raw = solve_rows(m_c, gram_a, gram_b, ridge)
            c_loc, gram_c, col_norms = normalise(c_raw, lax.psum(gram_part(c_raw), ALL_AXES))
        return a_loc, b_loc, c_loc, col_norms

    return jax.shard_map(
        body,
        mesh=mesh,
        in_specs=(P('ix', 'jy', 'kz'), P(('jy', 'ix', 'kz'), None), P(('kz', 'ix', 'jy'), None), P()),
        out_specs=(P(('ix', 'jy', 'kz'), None), P(('jy', 'ix', 'kz'), None), P(('kz', 'ix', 'jy'), None), P(None)),
        check_vma=False,
    )
```

profile of v0, /device:TPU:1, one launch (start us, length us, event | category | flops | bytes accessed | tf_op | source)
XLA Modules:
  0.0 1981.0 jit_solution(14097388555692030081)
XLA Ops:
  7.9 1.0 convolution_bitcast_fusion.2
  9.0 0.8 multiply_bitcast_fusion
  9.8 69.0 %psum.49 = f32[2,64,64]{2,1,0:T(8,128)S(1)} all-reduce(f32[2,64,64]{2,1,0:T(8,128)S(1)} %pad_maximum_fusion), channel_id=1, replica_groups=mesh['kz'=4,'jy'=4,'ix'=8] {'kz','jy','ix'}, use_global_device_ids=true, to_apply=%region_1.0 | all-reduce | flops 8192 | bytes 65536 | tf_op jit(solution)/shard_map/psum | solution.py:52
  78.8 99.8 %while.114 = (s32[]{:T(128)}, f32[64,64]{1,0:T(8,128)S(1)}, f32[64,64]{1,0:T(8,128)S(1)}, s32[]{:T(128)}, s32[]{:T(128)}, /*index=5*/s32[]{:T(128)}) while((s32[]{:T(128)}, f32[64,64]{1,0:T(8,128)S(1)}, f32[64,64]{1,0:T(8,128)S(1)}, s32[]{:T(128)}, s32[]{:T(128)}, /*index=5*/s32[]{:T(128)}) %tuple.272), condition=%wide.region_3.4_spmd.clone, body=%wide.region_2.3_spmd.clone.sunk | while | flops 24771 | bytes 68089 | solution.py:35
  79.4 0.7 fusion.103
  80.9 0.7 fusion.103
  178.6 41.3 %all-gather.3 = f32[32,1,64]{2,1,0:T(1,128)S(1)} all-gather(f32[1,1,64]{2,1,0:T(1,128)} %bitcast.209), channel_id=1, replica_groups=mesh['kz'=4,'jy'=4,'ix'=8] {'ix','kz'}, dimensions={0}, use_global_device_ids=true | all-gather | bytes 8448 | tf_op jit(solution)/shard_map/all_gather | solution.py:55
  219.9 41.5 %all-gather.2 = f32[32,12,64]{2,1,0:T(8,128)S(1)} all-gather(f32[1,12,64]{2,1,0:T(8,128)} %bitcast.204), channel_id=1, replica_groups=mesh['kz'=4,'jy'=4,'ix'=8] {'ix','jy'}, dimensions={0}, use_global_device_ids=true | all-gather | bytes 101376 | tf_op jit(solution)/shard_map/all_gather | solution.py:59
  261.5 11.8 multiply_reduce_fusion.1
  273.3 1.0 copy.24
  274.3 58.0 %all-reduce.2 = f32[192,64]{0,1:T(8,128)S(1)} all-reduce(f32[192,64]{0,1:T(8,128)S(1)} %bitcast.202), channel_id=4, replica_groups=mesh['kz'=4,'jy'=4,'ix'=8] {'jy','kz'}, use_global_device_ids=true, to_apply=%region_0.0.clone | all-reduce | flops 12288 | bytes 98304
  334.0 78.2 %psum.50 = f32[64,64]{1,0:T(8,128)S(1)} all-reduce(f32[64,64]{1,0:T(8,128)S(1)} %fusion.68), channel_id=1, replica_groups=mesh['kz'=4,'jy'=4,'ix'=8] {'kz','jy','ix'}, use_global_device_ids=true, to_apply=%region_4.5 | all-reduce | flops 4096 | bytes 32768 | tf_op jit(solution)/shard_map/psum | solution.py:64
  412.2 0.8 gather_fusion
  413.1 15.9 all-gather.4
  429.7 99.8 %while.115 = (s32[]{:T(128)}, f32[64,64]{1,0:T(8,128)S(1)}, f32[64,64]{1,0:T(8,128)S(1)}, s32[]{:T(128)}, s32[]{:T(128)}, /*index=5*/s32[]{:T(128)}) while((s32[]{:T(128)}, f32[64,64]{1,0:T(8,128)S(1)}, f32[64,64]{1,0:T(8,128)S(1)}, s32[]{:T(128)}, s32[]{:T(128)}, /*index=5*/s32[]{:T(128)}) %tuple.275), condition=%wide.region_7.8_spmd.clone, body=%wide.region_6.7_spmd.clone.sunk | while | flops 24771 | bytes 68089 | solution.py:35
  529.8 126.4 %all-reduce.3 = f32[32,64]{1,0:T(8,128)S(1)} all-reduce(f32[32,64]{1,0:T(8,128)S(1)} %bitcast.206), channel_id=5, replica_groups=mesh['kz'=4,'jy'=4,'ix'=8] {'ix','kz'}, use_global_device_ids=true, to_apply=%region_5.6.clone | all-reduce | flops 2048 | bytes 16384
  656.9 0.8 convolution_bitcast_fusion.4
  657.7 66.6 %psum.51 = f32[64,64]{1,0:T(8,128)S(1)} all-reduce(f32[64,64]{1,0:T(8,128)S(1)} %broadcast_multiply_fusion.1), channel_id=1, replica_groups=mesh['kz'=4,'jy'=4,'ix'=8] {'kz','jy','ix'}, use_global_device_ids=true, to_apply=%region_8.9 | all-reduce | flops 4096 | bytes 32768 | tf_op jit(solution)/shard_map/psum | solution.py:69
  724.3 0.8 gather_fusion.1
  725.1 1.0 copy.31
  726.9 61.8 %all-reduce = f32[2048]{0:T(1024)S(1)} all-reduce(f32[2048]{0:T(1024)S(1)} %get-tuple-element.865), channel_id=2, replica_groups=mesh['kz'=4,'jy'=4,'ix'=8] {'ix','kz'}, use_global_device_ids=true, to_apply=%add | all-reduce | flops 2048 | bytes 16384
  788.7 17.7 convolution_bitcast_fusion.1
  806.4 18.8 fusion.38
  826.0 99.8 %while.116 = (s32[]{:T(128)}, f32[64,64]{1,0:T(8,128)S(1)}, f32[64,64]{1,0:T(8,128)S(1)}, s32[]{:T(128)}, s32[]{:T(128)}, /*index=5*/s32[]{:T(128)}) while((s32[]{:T(128)}, f32[64,64]{1,0:T(8,128)S(1)}, f32[64,64]{1,0:T(8,128)S(1)}, s32[]{:T(128)}, s32[]{:T(128)}, /*index=5*/s32[]{:T(128)}) %tuple.278), condition=%wide.region_11.12_spmd.clone, body=%wide.region_10.11_spmd.clone.sunk | while | flops 24771 | bytes 68089 | solution.py:35
  927.3 1.1 fusion.52
  928.7 66.3 %psum.52 = f32[64,64]{1,0:T(8,128)S(1)} all-reduce(f32[64,64]{1,0:T(8,128)S(1)} %fusion.69), channel_id=1, replica_groups=mesh['kz'=4,'jy'=4,'ix'=8] {'kz','jy','ix'}, use_global_device_ids=true, to_apply=%region_12.13 | all-reduce | flops 4096 | bytes 32768 | tf_op jit(solution)/shard_map/psum | solution.py:75
  995.0 0.8 gather_fusion.2
  995.9 99.7 %while.117 = (s32[]{:T(128)}, f32[64,64]{1,0:T(8,128)S(1)}, f32[64,64]{1,0:T(8,128)S(1)}, s32[]{:T(128)}, s32[]{:T(128)}, /*index=5*/s32[]{:T(128)}) while((s32[]{:T(128)}, f32[64,64]{1,0:T(8,128)S(1)}, f32[64,64]{1,0:T(8,128)S(1)}, s32[]{:T(128)}, s32[]{:T(128)}, /*index=5*/s32[]{:T(128)}) %tuple.281), condition=%wide.region_15.16_spmd.clone, body=%wide.region_14.15_spmd.clone.sunk | while | flops 24771 | bytes 68089 | solution.py:35
  1095.7 41.9 %all-gather.5 = f32[32,12,64]{2,1,0:T(8,128)S(1)} all-gather(f32[1,12,64]{2,1,0:T(8,128)S(1)} %divide_bitcast_fusion), channel_id=1, replica_groups=mesh['kz'=4,'jy'=4,'ix'=8] {'ix','jy'}, dimensions={0}, use_global_device_ids=true | all-gather | bytes 101376 | tf_op jit(solution)/shard_map/all_gather | solution.py:59
  1137.6 18.3 fusion.40
  1155.8 2.3 fusion.42
  1158.1 57.7 %all-reduce.5 = f32[192,64]{0,1:T(8,128)S(1)} all-reduce(f32[192,64]{0,1:T(8,128)S(1)} %bitcast.203), channel_id=7, replica_groups=mesh['kz'=4,'jy'=4,'ix'=8] {'jy','kz'}, use_global_device_ids=true, to_apply=%region_13.14.clone | all-reduce | flops 12288 | bytes 98304
  1216.4 76.2 %psum.53 = f32[64,64]{1,0:T(8,128)S(1)} all-reduce(f32[64,64]{1,0:T(8,128)S(1)} %fusion.70), channel_id=1, replica_groups=mesh['kz'=4,'jy'=4,'ix'=8] {'kz','jy','ix'}, use_global_device_ids=true, to_apply=%region_16.17 | all-reduce | flops 4096 | bytes 32768 | tf_op jit(solution)/shard_map/psum | solution.py:64
  1292.6 0.8 gather_fusion.3
  1293.5 16.1 all-gather.6
  1309.6 99.8 %while.118 = (s32[]{:T(128)}, f32[64,64]{1,0:T(8,128)S(1)}, f32[64,64]{1,0:T(8,128)S(1)}, s32[]{:T(128)}, s32[]{:T(128)}, /*index=5*/s32[]{:T(128)}) while((s32[]{:T(128)}, f32[64,64]{1,0:T(8,128)S(1)}, f32[64,64]{1,0:T(8,128)S(1)}, s32[]{:T(128)}, s32[]{:T(128)}, /*index=5*/s32[]{:T(128)}) %tuple.295), condition=%wide.region_19.20_spmd.clone, body=%wide.region_18.19_spmd.clone.sunk | while | flops 24771 | bytes 68089 | solution.py:35
  1409.9 126.4 %all-reduce.6 = f32[32,64]{1,0:T(8,128)S(1)} all-reduce(f32[32,64]{1,0:T(8,128)S(1)} %bitcast.207), channel_id=8, replica_groups=mesh['kz'=4,'jy'=4,'ix'=8] {'ix','kz'}, use_global_device_ids=true, to_apply=%region_17.18.clone | all-reduce | flops 2048 | bytes 16384
  1536.3 0.8 convolution_bitcast_fusion.3
  1537.2 66.6 %psum.54 = f32[64,64]{1,0:T(8,128)S(1)} all-reduce(f32[64,64]{1,0:T(8,128)S(1)} %broadcast_multiply_fusion), channel_id=1, replica_groups=mesh['kz'=4,'jy'=4,'ix'=8] {'kz','jy','ix'}, use_global_device_ids=true, to_apply=%region_20.21 | all-reduce | flops 4096 | bytes 32768 | tf_op jit(solution)/shard_map/psum | solution.py:69
  1603.8 0.8 gather_fusion.4
  1605.3 99.8 %while.119 = (s32[]{:T(128)}, f32[64,64]{1,0:T(8,128)S(1)}, f32[64,64]{1,0:T(8,128)S(1)}, s32[]{:T(128)}, s32[]{:T(128)}, /*index=5*/s32[]{:T(128)}) while((s32[]{:T(128)}, f32[64,64]{1,0:T(8,128)S(1)}, f32[64,64]{1,0:T(8,128)S(1)}, s32[]{:T(128)}, s32[]{:T(128)}, /*index=5*/s32[]{:T(128)}) %tuple.294), condition=%wide.region_23.24_spmd.clone, body=%wide.region_22.23_spmd.clone.sunk | while | flops 24771 | bytes 68089 | solution.py:35
  1705.2 61.5 %all-reduce.1 = f32[2048]{0:T(1024)S(1)} all-reduce(f32[2048]{0:T(1024)S(1)} %get-tuple-element.862), channel_id=3, replica_groups=mesh['kz'=4,'jy'=4,'ix'=8] {'ix','kz'}, use_global_device_ids=true, to_apply=%add.1 | all-reduce | flops 2048 | bytes 16384
  1766.8 17.7 convolution_bitcast_fusion
  1784.4 19.0 fusion.36
  1804.7 100.5 %all-reduce.13.cloned.1.call-done = f32[384,64]{0,1:T(8,128)} async-done(((f32[384,64]{0,1:T(8,128)}), f32[384,64]{0,1:T(8,128)}) %all-reduce.13.cloned.1.call-update) | async-done | bytes 98320
  1905.2 1.1 fusion.48
  1906.6 65.7 %psum.55 = f32[64,64]{1,0:T(8,128)S(1)} all-reduce(f32[64,64]{1,0:T(8,128)S(1)} %fusion.71), channel_id=1, replica_groups=mesh['kz'=4,'jy'=4,'ix'=8] {'kz','jy','ix'}, use_global_device_ids=true, to_apply=%region_24.25 | all-reduce | flops 4096 | bytes 32768 | tf_op jit(solution)/shard_map/psum | solution.py:75
  1972.2 0.8 gather_fusion.5
  (1990 shorter events, 590.0 us)
Async XLA Ops:
  7.2 325.1 %copy-start.6 = (u32[128]{0:T(128)S(1)}, u32[128]{0:T(128)}, u32[]{:S(2)}) copy-start(u32[128]{0:T(128)} %constant.584) | copy-start | bytes 1540
  7.2 920.1 %all-reduce.11.cloned.1.call-start = ((), (), s32[]{:S(2)}) async-start(), calls=%async_computation | async-start | bytes 196608
  7.2 918.7 %copy-start = (f32[64,64]{1,0:T(8,128)}, f32[64,64]{1,0:T(8,128)S(1)}, u32[]{:S(2)}) copy-start(f32[64,64]{1,0:T(8,128)S(1)} %fusion.56) | copy-start | bytes 49156
  261.4 394.8 %copy-start.3 = (u32[128]{0:T(128)S(1)}, u32[128]{0:T(128)}, u32[]{:S(2)}) copy-start(u32[128]{0:T(128)} %constant.569) | copy-start | bytes 1540
  806.4 119.5 %copy-start.5 = (u32[128]{0:T(128)S(1)}, u32[128]{0:T(128)}, u32[]{:S(2)}) copy-start(u32[128]{0:T(128)} %constant.592) | copy-start | bytes 1540
  825.9 1079.3 %all-reduce.13.cloned.1.call-start = ((), (), s32[]{:S(2)}) async-start(), calls=%async_computation.1 | async-start | bytes 196608
  925.9 383.7 %copy-start.2 = (f32[64,64]{1,0:T(8,128)S(1)}, f32[64,64]{1,0:T(8,128)}, u32[]{:S(2)}) copy-start(f32[64,64]{1,0:T(8,128)} %copy-done) | copy-start | bytes 49156
  1137.6 467.7 %copy-start.1 = (f32[64,64]{1,0:T(8,128)S(1)}, f32[64,64]{1,0:T(8,128)}, u32[]{:S(2)}) copy-start(f32[64,64]{1,0:T(8,128)} %copy-done) | copy-start | bytes 49156
  1973.1 0.6 copy-start.4
Sparse Core Ops, SparseCore 0:
  826.0 101.2 all-reduce.10
  1804.2 100.9 all-reduce.12
where the time goes:
time: 1990 us; the launch traced here: 1980 us
  blocking collectives  1140 us (57%)
  local copies, waits for them, and re-layouts  304 us (15%)
  other arithmetic  293 us (15%)
  matrix products  112 us (6%)
  waiting for transfers between devices  101 us (5%)
    unnamed x6, blocking collectives  492 us
    broadcast_in_dim x384, other arithmetic, value_a9(): right_mat = jnp.where(is_pivot, row_right, right_mat - col_vals * row_right)  251 us
    dynamic_slice x384, local copies, waits for them, and re-layouts, value_a9(): pivot_val = lax.dynamic_slice_in_dim(pivot_left, col_idx, 1, axis=1)  226 us
    psum x2, blocking collectives, body(): lax.psum(gram_part(a_raw), ALL_AXES)  154 us
    psum x2, blocking collectives, body(): lax.psum(gram_part(b_raw), ALL_AXES)  133 us
    psum x2, blocking collectives, body(): lax.psum(gram_part(c_raw), ALL_AXES)  132 us
    dot_general x18, matrix products, mat_prod(): jnp.einsum(form, left, right, precision=lax.Precision.HIGHEST, preferred_...  112 us
    unnamed x4, waiting for transfers between devices  101 us
  transfers between devices with their start and end apart: 2, of which 2 were waited for; matrix products, arithmetic and copies ran while one was open for 5% of the time, Pallas kernels for 0%

commit v1 on v0

v1 whole, which is shorter than its diff:
```python
import functools

import jax
import jax.numpy as jnp
from jax import lax
from jax.experimental import pallas as pl
from jax.experimental.pallas import tpu as pltpu
from jax.sharding import PartitionSpec as P

MESH = pl.DeviceIdType.MESH
F32 = jnp.float32
BF16 = jnp.bfloat16
SWEEPS = 2
RANK = 64
LANES = 128
CHUNKS = 8
GRAM_ROWS = 40


def full_dot(left, right):
    return jnp.dot(left, right, precision=lax.Precision.HIGHEST, preferred_element_type=F32)


def full_dot_nt(left, right):
    return lax.dot_general(left, right, (((1,), (1,)), ((), ())), precision=lax.Precision.HIGHEST, preferred_element_type=F32)


def piece_dot(left, right):
    return jnp.dot(left, right, preferred_element_type=F32)


def split3(value):
    high = value.astype(BF16)
    rest = value - high.astype(F32)
    mid = rest.astype(BF16)
    low = (rest - mid.astype(F32)).astype(BF16)
    return high, mid, low


def iota(shape, dim):
    return lax.broadcasted_iota(jnp.int32, shape, dim)


def left_half(shape):
    return iota(shape, 1) < RANK


def swap_halves(value):
    return pltpu.roll(value, RANK, 1)


def pack_dup(dup):
    half = dup.shape[0] // 2
    return jnp.where(left_half((half, LANES)), dup[:half], dup[half:])


def unpack_dup(packed):
    swapped = swap_halves(packed)
    is_left = left_half(packed.shape)
    return jnp.concatenate([jnp.where(is_left, packed, swapped), jnp.where(is_left, swapped, packed)], axis=0)


def eye_mask():
    return iota((RANK, LANES), 0) == iota((RANK, LANES), 1)


def diag_row(gram):
    return jnp.sum(jnp.where(eye_mask(), gram, 0.0), axis=0, keepdims=True)


def diag_col(gram):
    return jnp.sum(jnp.where(eye_mask(), gram, 0.0), axis=1, keepdims=True)


def eliminate(state):
    rows = iota((RANK, LANES), 0)
    for t in range(8):
        col = jnp.broadcast_to(state[:, t:t + 1], (RANK, LANES))
        row = state[t:t + 1, :] / col[t:t + 1, :]
        state = jnp.where(rows == t, row, state - col * row)
    state = jnp.concatenate([state[8:], state[:8]], axis=0)
    return pltpu.roll(state, LANES - 8, 1)


class Links:
    def __init__(self, send_sem, recv_sem):
        self.send_sem, self.recv_sem = send_sem, recv_sem
        self.used = 0
        self.sent = []

    def copy(self, src, dst, device):
        n = self.used
        self.used += 1
        desc = pltpu.make_async_remote_copy(
            src_ref=src, dst_ref=dst, send_sem=self.send_sem.at[n], recv_sem=self.recv_sem.at[n],
            device_id=device, device_id_type=MESH)
        desc.start()
        self.sent.append(desc)
        return desc

    def drain(self):
        for desc in self.sent:
            desc.wait_send()


def count_copies(nx, ny, nz):
    x, y, z = nx - 1, ny - 1, nz - 1
    a = 2 * (y + z)
    b = 1 + 2 * (x + z)
    c = 2 + 2 * (x + y)
    return SWEEPS * a + (SWEEPS + 1) * (b + c) + (SWEEPS + 1) * (y + z) + SWEEPS * (1 + x) + 1 + x


def kernel(sizes, x_hbm, b_in, c_in, lam_ref, a_out, b_out, c_out, w_out,
           x_stage, x_hi, x_mid, x_low, t_ref, pa_ref, a_dup, a_pack, acc_ref, b_pad, c_pad, inv_ref,
           a_buf, b_core, b_buf, c_part, c_rs, c_buf, ct_ref, g_core, g_buf, s_core, s_buf,
           load_sem, send_sem, recv_sem):
    nx, ny, nz = sizes
    kz, jy, ix = lax.axis_index("kz"), lax.axis_index("jy"), lax.axis_index("ix")
    xx, core = lax.div(ix, 2), lax.rem(ix, 2)
    where = {"x": xx, "y": jy, "z": kz}
    count = {"x": nx, "y": ny, "z": nz}

    def peer(axis, d):
        if axis == "x":
            return {"ix": 2 * lax.rem(xx + d, nx) + core}
        if axis == "y":
            return {"jy": lax.rem(jy + d, ny)}
        return {"kz": lax.rem(kz + d, nz)}

    partner = {"ix": 2 * xx + (1 - core)}
    links = Links(send_sem, recv_sem)

    rows_x, width = x_stage.shape
    rows_i = rows_x // b_buf_rows(b_core)
    rows_j = 2 * b_core.shape[2]
    step = rows_x // CHUNKS

    loads = [
        pltpu.make_async_copy(x_hbm.at[pl.ds(n * step, step)], x_stage.at[pl.ds(n * step, step)], load_sem.at[n])
        for n in range(CHUNKS)
    ]
    for load in loads:
        load.start()

    barrier = pltpu.get_barrier_semaphore()
    others = [partner] + [peer(axis, d) for axis in "xyz" for d in range(1, count[axis])]
    for other in others:
        pl.semaphore_signal(barrier, inc=1, device_id=other, device_id_type=MESH)
    pl.semaphore_wait(barrier, len(others))

    def spread(slots, axis):
        mine = slots.at[where[axis]]
        return [links.copy(mine, mine, peer(axis, d)) for d in range(1, count[axis])]

    def gather(slots, axis, copies, op=jnp.add):
        for desc in copies:
            desc.wait_recv()
        total = slots[0]
        for n in range(1, count[axis]):
            total = op(total, slots[n])
        return total

    class PlaneSum:
        def __init__(self, buf, axes):
            self.buf = buf
            self.orders = (axes, axes[::-1])

        def start(self, halves):
            self.copies = []
            for h, half in enumerate(halves):
                first = self.orders[h][0]
                slots = self.buf.at[0, h]
                slots[where[first]] = half
                self.copies.append(spread(slots, first))

        def turn(self):
            copies, self.copies = self.copies, []
            for h in range(2):
                first, second = self.orders[h]
                total = gather(self.buf.at[0, h], first, copies[h])
                slots = self.buf.at[1, h]
                slots[where[second]] = total
                self.copies.append(spread(slots, second))

        def finish(self):
            return jnp.concatenate(
                [gather(self.buf.at[1, h], self.orders[h][1], self.copies[h]) for h in range(2)], axis=0)

    def halves_of(value):
        half = value.shape[0] // 2
        return value[:half], value[half:]

    class SumA(PlaneSum):
        def __init__(self, n):
            super().__init__(a_buf.at[n], "yz")

    class SumB(PlaneSum):
        def __init__(self, n):
            super().__init__(b_buf.at[n], "xz")
            self.pair = b_core.at[n]

        def begin(self, packed):
            self.pair[core] = packed
            self.pair_copy = links.copy(self.pair.at[core], self.pair.at[core], partner)

        def join(self):
            self.pair_copy.wait_recv()
            self.start(halves_of(self.pair[0] + self.pair[1]))

    class SumC(PlaneSum):
        def __init__(self, n):
            super().__init__(c_buf.at[n], "xy")
            self.part, self.got, self.ct = c_part.at[n], c_rs.at[n], ct_ref.at[n]

        def begin(self, part):
            self.part[...] = part
            self.pair_copy = links.copy(self.part.at[pl.ds(pl.multiple_of(32 * (1 - core), 32), 32)], self.got, partner)

        def join(self):
            self.pair_copy.wait_recv()
            self.start(halves_of(self.part[pl.ds(pl.multiple_of(32 * core, 32), 32), :] + self.got[...]))

        def share(self):
            mine = pl.ds(pl.multiple_of(32 * core, 32), 32)
            self.ct[mine, :] = self.finish()
            self.pair_copy = links.copy(self.ct.at[mine], self.ct.at[mine], partner)

        def result(self):
            self.pair_copy.wait_recv()
            return self.ct[...]

    class GramSum:
        def __init__(self, n, axis):
            self.slots, self.axis = g_buf.at[n], axis

        def start(self, packed, tile=None):
            mine = where[self.axis]
            self.slots[mine, 0:32] = packed
            self.slots[mine, 32:GRAM_ROWS] = jnp.zeros((8, LANES), F32) if tile is None else tile
            self.copies = spread(self.slots, self.axis)

        def finish(self):
            for desc in self.copies:
                desc.wait_recv()
            total, peak = self.slots[0, 0:32], self.slots[0, 32:GRAM_ROWS]
            for n in range(1, count[self.axis]):
                total = total + self.slots[n, 0:32]
                peak = jnp.maximum(peak, self.slots[n, 32:GRAM_ROWS])
            return unpack_dup(total), peak

    class GramSumA(GramSum):
        def __init__(self, n, m):
            super().__init__(n, "x")
            self.pair = g_core.at[m]

        def begin(self, packed):
            self.pair[core] = packed
            self.pair_copy = links.copy(self.pair.at[core], self.pair.at[core], partner)

        def join(self):
            self.pair_copy.wait_recv()
            self.start(self.pair[0] + self.pair[1])

    def gram_of_packed(packed):
        prod = full_dot(jnp.transpose(packed), packed)
        gram = prod[:RANK] + swap_halves(prod[RANK:])
        return jnp.where(left_half((32, LANES)), gram[:32], swap_halves(gram[32:]))

    def gram_of_ct(ct):
        gram = full_dot_nt(ct, jnp.concatenate([ct, ct], axis=0))
        return jnp.where(left_half((32, LANES)), gram[:32], gram[32:])

    nb, nc, na = b_in.shape[0], c_in.shape[0], a_out.shape[0]
    b_pad[...] = jnp.zeros_like(b_pad)
    c_pad[...] = jnp.zeros_like(c_pad)
    b_pad[0:nb, 0:RANK] = b_in[...]
    c_pad[0:nc, 0:RANK] = c_in[...]
    b_base = (ix * nz + kz) * nb
    c_base = (ix * ny + jy) * nc
    a_base = (jy * nz + kz) * na

    def chooser(base, used, size, pad):
        t = iota((pad, size), 0)
        return jnp.where((iota((pad, size), 1) == t + base) & (t < used), 1.0, 0.0).astype(F32)

    b_own = b_pad[...] + swap_halves(b_pad[...])
    b_rows = full_dot(jnp.transpose(chooser(b_base, nb, rows_j, b_pad.shape[0])), b_own)
    sum_b = SumB(0)
    sum_b.begin(pack_dup(b_rows))
    sum_c = SumC(0)
    sum_c.begin(full_dot(jnp.transpose(c_pad[...]), chooser(c_base, nc, width, c_pad.shape[0]))[:RANK])

    sub = 64

    def split_rows(n, peak):
        rows = pl.ds(pl.multiple_of(n * sub, sub), sub)
        value = x_stage[rows, :]
        high, mid, low = split3(value)
        x_hi[rows, :] = high
        x_mid[rows, :] = mid
        x_low[rows, :] = low
        size = jnp.abs(value)
        for m in range(sub // 8):
            for q in range(width // LANES):
                peak = jnp.maximum(peak, size[m * 8:m * 8 + 8, q * LANES:(q + 1) * LANES])
        return peak

    def split_chunks(lo, hi, peak):
        for n in range(lo, hi):
            loads[n].wait()
            peak = lax.fori_loop(n * step // sub, (n + 1) * step // sub, split_rows, peak)
        return peak

    peak = split_chunks(0, 2, jnp.zeros((8, LANES), F32))
    sum_c.join()
    sum_b.join()
    peak = split_chunks(2, CHUNKS, peak)
    s_core[core] = peak
    s_copy = links.copy(s_core.at[core], s_core.at[core], partner)
    sum_c.turn()
    sum_b.turn()
    s_copy.wait_recv()
    s_buf[xx] = jnp.maximum(s_core[0], s_core[1])
    s_copies = spread(s_buf, "x")
    sum_c.share()
    b_pack = sum_b.finish()
    b_dup = unpack_dup(b_pack)
    peak = gather(s_buf, "x", s_copies, jnp.maximum)
    gram_sum_b = GramSum(0, "y")
    gram_sum_b.start(gram_of_packed(b_pack), peak)
    ct = sum_c.result()
    gram_b, peak = gram_sum_b.finish()
    gram_sum_c = GramSum(1, "z")
    gram_sum_c.start(gram_of_ct(ct), peak)

    inv_b_row = jnp.ones((1, LANES), F32)
    inv_b_col = jnp.ones((RANK, 1), F32)

    def inv_norms(gram):
        return 1.0 / jnp.sqrt(diag_row(gram)), 1.0 / jnp.sqrt(diag_col(gram))

    def system(gram_one, gram_two, row_scale, col_scale):
        row_wide = row_scale + swap_halves(row_scale)
        ridge = jnp.where(eye_mask(), lam_ref[0, 0], 0.0)
        mat = gram_one * gram_two * row_wide * col_scale + ridge
        unit = jnp.where(iota((RANK, LANES), 0) + RANK == iota((RANK, LANES), 1), 1.0, 0.0)
        inv_ref[...] = jnp.where(left_half((RANK, LANES)), mat, unit)

    def invert(lo, hi):
        inv_ref[...] = lax.fori_loop(lo, hi, lambda n, state: eliminate(state), inv_ref[...])

    def inverse():
        return jnp.where(left_half((RANK, LANES)), inv_ref[...], 0.0)

    def twice(mat):
        return jnp.concatenate([mat, swap_halves(mat)], axis=0)

    inv_c_row = inv_c_col = None
    inv_s = None
    for sweep in range(SWEEPS):
        wide = jnp.transpose(jnp.concatenate([ct, ct], axis=0))
        c_hi, c_mid, c_low = split3(wide)
        c_hi, c_mid, c_low = c_hi.astype(F32), c_mid.astype(F32), c_low.astype(F32)
        is_left = left_half(wide.shape)
        none = jnp.zeros_like(wide)
        w_hi = jnp.concatenate([jnp.where(is_left, c_hi, c_mid), jnp.where(is_left, c_low, none)], axis=1).astype(BF16)
        w_mid = jnp.concatenate([jnp.where(is_left, none, c_hi), jnp.where(is_left, c_mid, none)], axis=1).astype(BF16)
        w_low = jnp.concatenate([none, jnp.where(is_left, c_hi, none)], axis=1).astype(BF16)
        per = 16

        def t_step(n, unused, w_hi=w_hi, w_mid=w_mid, w_low=w_low, b_dup=b_dup):
            rows = pl.ds(pl.multiple_of(n * per * rows_j, per * rows_j), per * rows_j)
            prod = piece_dot(x_hi[rows, :], w_hi) + piece_dot(x_mid[rows, :], w_mid) + piece_dot(x_low[rows, :], w_low)
            t_val = prod[:, :LANES] + prod[:, LANES:]
            t_ref[rows, :] = t_val
            part = jnp.sum(t_val.reshape(per, rows_j, LANES) * b_dup[None], axis=1)
            pa_ref[pl.ds(pl.multiple_of(n * per, per), per), :] = part
            return unused

        lax.fori_loop(0, rows_i // per, t_step, 0)
        part = pa_ref[...]
        part = part + swap_halves(part)
        sum_a = SumA(sweep)
        sum_a.start(halves_of(pack_dup(part)))
        gram_c, top = gram_sum_c.finish()
        if sweep == 0:
            inv_c_row, inv_c_col = inv_b_row, inv_b_col
            inv_s = 1.0 / jnp.max(top, axis=(0, 1), keepdims=True)
            top_all = jnp.max(top, axis=(0, 1), keepdims=True)
            row_scale = jnp.where(left_half((1, LANES)), 1.0, 0.0)
            col_scale = jnp.ones((RANK, 1), F32)
        else:
            inv_c_row, inv_c_col = inv_norms(gram_c)
            row_scale, col_scale = inv_b_row * inv_c_row, inv_b_col * inv_c_col
        row_scale = jnp.where(left_half((1, LANES)), row_scale, 0.0)
        system(gram_b, gram_c, row_scale, col_scale)
        invert(0, 4)
        sum_a.turn()
        invert(4, 8)
        solver = twice(inverse() * (col_scale * inv_s))
        a_val = full_dot(sum_a.finish(), solver)
        a_pack[...] = a_val
        a_dup[...] = unpack_dup(a_val)
        gram_sum_a = GramSumA(2 + 3 * sweep, sweep)
        pad8 = jnp.zeros((8, LANES), F32)
        gram_sum_a.begin(gram_of_packed(a_val))
        def b_step(n, total):
            rows = pl.ds(pl.multiple_of(n * per * rows_j, per * rows_j), per * rows_j)
            t_val = t_ref[rows, :].reshape(per, rows_j, LANES)
            a_val = a_dup[pl.ds(pl.multiple_of(n * per, per), per), :]
            for m in range(per):
                total = total + t_val[m] * a_val[m:m + 1, :]
            return total

        part = lax.fori_loop(0, rows_i // per, b_step, jnp.zeros((rows_j, LANES), F32))
        part = part + swap_halves(part)
        sum_b = SumB(1 + sweep)
        sum_b.begin(pack_dup(part))
        gram_sum_a.join()
        sum_b.join()
        gram_a, unused_top = gram_sum_a.finish()
        inv_a_row, inv_a_col = inv_norms(gram_a)
        inv_a_row = jnp.where(left_half((1, LANES)), inv_a_row, 0.0)
        if sweep == 0:
            row_scale, col_scale = inv_a_row, inv_a_col
        else:
            row_scale, col_scale = inv_a_row * inv_c_row, inv_a_col * inv_c_col
        row_scale = jnp.where(left_half((1, LANES)), row_scale, 0.0)
        system(gram_a, gram_c, row_scale, col_scale)
        sum_b.turn()
        invert(0, 8)
        solver = twice(inverse() * (col_scale * inv_s))
        b_pack = full_dot(sum_b.finish(), solver)
        b_dup = unpack_dup(b_pack)
        gram_sum_b = GramSum(3 + 3 * sweep, "y")
        gram_sum_b.start(gram_of_packed(b_pack))
        acc_ref[...] = jnp.zeros_like(acc_ref)
        grp = 8

        def c_step(n, unused, b_dup=b_dup):
            a_val = a_pack[pl.ds(pl.multiple_of(n * grp, grp), grp), :]
            prod = jnp.concatenate([a_val[m:m + 1, :] * b_dup for m in range(grp)], axis=0)
            high, mid, low = split3(jnp.transpose(prod))
            for h in range(2):
                start = n * grp * rows_j + h * (rows_x // 2)
                rows = pl.ds(pl.multiple_of(start, grp * rows_j), grp * rows_j)
                side = slice(h * RANK, (h + 1) * RANK)
                left = jnp.concatenate([high[side], mid[side], low[side]], axis=0)
                acc_ref[...] += piece_dot(left, x_hi[rows, :])
                acc_ref[0:2 * RANK, :] += piece_dot(left[:2 * RANK], x_mid[rows, :])
                acc_ref[0:RANK, :] += piece_dot(left[:RANK], x_low[rows, :])
            return unused

        lax.fori_loop(0, rows_i // 2 // grp, c_step, 0)
        sum_c = SumC(1 + sweep)
        sum_c.begin(acc_ref[0:RANK, :] + acc_ref[RANK:2 * RANK, :] + acc_ref[2 * RANK:, :])
        gram_b, unused_top = gram_sum_b.finish()
        inv_b_row, inv_b_col = inv_norms(gram_b)
        row_scale, col_scale = inv_a_row * inv_b_row, inv_a_col * inv_b_col
        row_scale = jnp.where(left_half((1, LANES)), row_scale, 0.0)
        system(gram_a, gram_b, row_scale, col_scale)
        sum_c.join()
        invert(0, 4)
        sum_c.turn()
        invert(4, 8)
        sum_c.share()
        solver = inverse() * (row_scale * inv_s)
        ct = full_dot(solver[:, :RANK], sum_c.result())
        gram_sum_c = GramSum(4 + 3 * sweep, "z")
        gram_sum_c.start(gram_of_ct(ct))

    a_rows = full_dot(chooser(a_base, na, rows_i, c_pad.shape[0] if na <= c_pad.shape[0] else na), a_dup[...]) * inv_a_row
    a_out[...] = a_rows[:na, :RANK]
    b_rows = full_dot(chooser(b_base, nb, rows_j, b_pad.shape[0]), b_dup) * inv_b_row
    b_out[...] = b_rows[:nb, :RANK]
    c_rows = full_dot_nt(chooser(c_base, nc, width, c_pad.shape[0]), ct)
    gram_c, unused_top = gram_sum_c.finish()
    norm_c = jnp.sqrt(diag_row(gram_c))
    c_out[...] = c_rows[:nc, :] / norm_c[:, :RANK]
    w_out[...] = (norm_c * top_all)[:, :RANK]
    links.drain()


def b_buf_rows(b_core):
    return 2 * b_core.shape[2]


def solution(mesh):
    nx, ny, nz = mesh.shape["ix"] // 2, mesh.shape["jy"], mesh.shape["kz"]
    sizes = (nx, ny, nz)

    def body(x_blk, b_loc, c_loc, ridge):
        rows_i, rows_j, width = x_blk.shape
        rows_x = rows_i * rows_j
        nb, nc, na = b_loc.shape[0], c_loc.shape[0], rows_i // (ny * nz)
        big = max(nx, ny, nz)
        copies = count_copies(nx, ny, nz)
        vmem = pl.BlockSpec(memory_space=pltpu.VMEM)
        up8 = lambda n: -(-n // 8) * 8
        up16 = lambda n: -(-n // 16) * 16
        outs = pl.pallas_call(
            functools.partial(kernel, sizes),
            out_shape=(
                jax.ShapeDtypeStruct((na, RANK), F32),
                jax.ShapeDtypeStruct((nb, RANK), F32),
                jax.ShapeDtypeStruct((nc, RANK), F32),
                jax.ShapeDtypeStruct((1, RANK), F32),
            ),
            in_specs=[pl.BlockSpec(memory_space=pl.ANY), vmem, vmem, pl.BlockSpec(memory_space=pltpu.SMEM)],
            out_specs=(vmem, vmem, vmem, vmem),
            scratch_shapes=[
                pltpu.VMEM((rows_x, width), F32),
                pltpu.VMEM((rows_x, width), BF16),
                pltpu.VMEM((rows_x, width), BF16),
                pltpu.VMEM((rows_x, width), BF16),
                pltpu.VMEM((rows_x, LANES), F32),
                pltpu.VMEM((rows_i, LANES), F32),
                pltpu.VMEM((rows_i, LANES), F32),
                pltpu.VMEM((rows_i // 2, LANES), F32),
                pltpu.VMEM((3 * RANK, width), F32),
                pltpu.VMEM((up8(nb), LANES), F32),
                pltpu.VMEM((up16(nc), LANES), F32),
                pltpu.VMEM((RANK, LANES), F32),
                pltpu.VMEM((SWEEPS, 2, 2, big, rows_i // 4, LANES), F32),
                pltpu.VMEM((SWEEPS + 1, 2, rows_j // 2, LANES), F32),
                pltpu.VMEM((SWEEPS + 1, 2, 2, big, rows_j // 4, LANES), F32),
                pltpu.VMEM((SWEEPS + 1, RANK, width), F32),
                pltpu.VMEM((SWEEPS + 1, RANK // 2, width), F32),
                pltpu.VMEM((SWEEPS + 1, 2, 2, big, RANK // 4, width), F32),
                pltpu.VMEM((SWEEPS + 1, RANK, width), F32),
                pltpu.VMEM((SWEEPS, 2, 32, LANES), F32),
                pltpu.VMEM((2 + 3 * SWEEPS, big, GRAM_ROWS, LANES), F32),
                pltpu.VMEM((2, 8, LANES), F32),
                pltpu.VMEM((big, 8, LANES), F32),
                pltpu.SemaphoreType.DMA((CHUNKS,)),
                pltpu.SemaphoreType.DMA((copies,)),
                pltpu.SemaphoreType.DMA((copies,)),
            ],
            compiler_params=pltpu.CompilerParams(collective_id=0, has_side_effects=True, vmem_limit_bytes=60 * 1024 * 1024),
            name="cp_als",
        )(x_blk.reshape(rows_x, width), b_loc, c_loc, ridge.reshape(1, 1))
        a_loc, b_new, c_new, weights = outs
        return a_loc, b_new, c_new, weights.reshape(RANK)

    return jax.shard_map(
        body,
        mesh=mesh,
        in_specs=(P('ix', 'jy', 'kz'), P(('jy', 'ix', 'kz'), None), P(('kz', 'ix', 'jy'), None), P()),
        out_specs=(P(('ix', 'jy', 'kz'), None), P(('jy', 'ix', 'kz'), None), P(('kz', 'ix', 'jy'), None), P(None)),
        check_vma=False,
    )
```

time: 1990 us -> 120 us (0.06)
  blocking collectives: 1140 us -> 0 us
  local copies, waits for them, and re-layouts: 304 us -> 4.91 us
  other arithmetic: 293 us -> 0 us
  Pallas kernels: 0 us -> 113 us
  matrix products: 112 us -> 0 us
  waiting for transfers between devices: 101 us -> 0 us
    unnamed x6 -> x0, blocking collectives: 492 us -> none
    psum x7 -> x0, blocking collectives: 488 us -> none  [the longest x2 154 us: body(): lax.psum(gram_part(a_raw), ALL_AXES)]
    dynamic_slice x768 -> x0, local copies, waits for them, and re-layouts: 293 us -> none  [the longest x384 226 us: value_a9(): pivot_val = lax.dynamic_slice_in_dim(pivot_left, col_idx, 1, axis=1)]
    broadcast_in_dim x384 -> x0, other arithmetic: 251 us -> none  [value_a9(): right_mat = jnp.where(is_pivot, row_right, right_mat - col_vals * row_right)]
    all_gather x5 -> x0, blocking collectives: 157 us -> none  [the longest x2 83.4 us: body(): c_rows = lax.all_gather(c_loc, ('ix', 'jy'), axis=0, tiled=True)]
    pallas_call x0 -> x1, Pallas kernels: none -> 113 us  [body(): pl.pallas_call(functools.partial(kernel, sizes), out_shape=(jax.ShapeDtyp...]
    dot_general x18 -> x0, matrix products: 112 us -> none  [mat_prod(): jnp.einsum(form, left, right, precision=lax.Precision.HIGHEST, preferred_...]
    unnamed x4 -> x0, waiting for transfers between devices: 101 us -> none
  transfers between devices with their start and end apart: 2 -> 0, of which waited for: 2 -> 0; matrix products, arithmetic and copies ran while one was open for 5% -> 0% of each run, Pallas kernels for 0% -> 0%
where the time goes in v1:
time: 120 us; the launch traced here: 119 us
  Pallas kernels  113 us (94%)
  local copies, waits for them, and re-layouts  4.91 us (4%)
  between operations  1.29 us (1%)
    pallas_call x1, Pallas kernels, body(): pl.pallas_call(functools.partial(kernel, sizes), out_shape=(jax.ShapeDtyp...  113 us
    unnamed x4, local copies, waits for them, and re-layouts  4.91 us

profile of v1, /device:TPU:1, one launch (start us, length us, event | category | flops | bytes accessed | tf_op | source)
XLA Modules:
  0.0 119.3 jit_solution(5197175930777612775)
XLA Ops:
  1.3 113.1 %cp_als.1 = (f32[12,64]{1,0:T(8,128)}, f32[1,64]{1,0:T(1,128)}, f32[12,64]{1,0:T(8,128)}, f32[1,64]{1,0:T(1,128)}) custom-call(f32[6144,384]{1,0:T(8,128)} %bitcast.4, f32[1,64]{1,0:T(1,128)} %b_in.1, f32[12,64]{1,0:T(8,128)} %c_in.1, f32[1,1]{1,0:T(1,128)} %bitcast.3.lam_ref), custom_call_target="tpu_custom_call" | custom-call | tf_op jit(solution)/shard_map/cp_als/pallas_call | solution.py:502
  114.4 1.3 %copy.13 = f32[12,64]{1,0:T(8,128)} copy(f32[12,64]{1,0:T(8,128)} %get-tuple-element.16) | data formatting | bytes 6144
  115.7 1.2 copy.14
  116.9 1.3 %copy.15 = f32[12,64]{1,0:T(8,128)} copy(f32[12,64]{1,0:T(8,128)} %get-tuple-element.18) | data formatting | bytes 6144
  118.2 1.1 copy.16
